TPU v7x, 128 devices: a whole 4x4x4 slice. The times are simulated.
128 devices in a mesh: tp: 64 (over z, y, x), dp: 2 (over core).
Axes of the slice: x: 4, y: 4, z: 4, core: 2. Of those that a mesh axis runs over, the one named last changes fastest.
Arguments:
- x_in: bfloat16 [128, 3072], P('dp')
- w_gate: bfloat16 [3072, 24576], P('dp', 'tp')
- w_up: bfloat16 [3072, 24576], P('dp', 'tp')
- w_down: bfloat16 [24576, 3072], P('tp', 'dp')
- dy_in: bfloat16 [128, 3072], P('dp')
Outputs:
- output 1: bfloat16 [128, 3072], P('dp')
- output 2: bfloat16 [128, 3072], P('dp')
- output 3: float32 [3072, 24576], P('dp', 'tp')
- output 4: float32 [3072, 24576], P('dp', 'tp')
- output 5: float32 [24576, 3072], P('tp', 'dp')
All inputs are finite; a program needn't handle non-finite values.
Results may differ from a plain program's by a relative error of at most 0.001.
Values are sent between devices in bfloat16 or wider.
A program may use at most 1 GiB of HBM per device.

v0:
```python
import jax
import jax.numpy as jnp
from jax import lax
from jax.sharding import PartitionSpec as P


def solution(mesh):
    def device_pass(x_rows, gate_blk, up_blk, down_blk, dy_rows):
        x_cols = lax.all_to_all(x_rows, 'dp', 1, 0, tiled=True)
        gate_part = jnp.dot(x_cols, gate_blk, preferred_element_type=jnp.float32)
        up_part = jnp.dot(x_cols, up_blk, preferred_element_type=jnp.float32)
        gate_pre = lax.psum_scatter(gate_part, 'dp', scatter_dimension=0, tiled=True)
        up_pre = lax.psum_scatter(up_part, 'dp', scatter_dimension=0, tiled=True)
        sig_gate = jax.nn.sigmoid(gate_pre)
        silu_gate = gate_pre * sig_gate
        hidden = (silu_gate * up_pre).astype(jnp.bfloat16)
        hidden_all = lax.all_gather(hidden, 'dp', axis=0, tiled=True)
        out_part = jnp.dot(hidden_all, down_blk, preferred_element_type=jnp.float32)
        y_cols = (x_cols.astype(jnp.float32) + lax.psum(out_part, 'tp')).astype(jnp.bfloat16)
        y_rows = lax.all_to_all(y_cols, 'dp', 0, 1, tiled=True)
        dy_cols = lax.all_to_all(dy_rows, 'dp', 1, 0, tiled=True)
        grad_part = jnp.einsum('td,fd->tf', dy_cols, down_blk, preferred_element_type=jnp.float32)
        grad_h = lax.psum_scatter(grad_part, 'dp', scatter_dimension=0, tiled=True)
        d_gate = (grad_h * up_pre * sig_gate * (1.0 + gate_pre * (1.0 - sig_gate))).astype(jnp.bfloat16)
        d_up = (grad_h * silu_gate).astype(jnp.bfloat16)
        gate_all = lax.all_gather(d_gate, 'dp', axis=0, tiled=True)
        up_all = lax.all_gather(d_up, 'dp', axis=0, tiled=True)
        dx_part = (jnp.einsum('tf,df->td', gate_all, gate_blk, preferred_element_type=jnp.float32)
                   + jnp.einsum('tf,df->td', up_all, up_blk, preferred_element_type=jnp.float32))
        dx_cols = (dy_cols.astype(jnp.float32) + lax.psum(dx_part, 'tp')).astype(jnp.bfloat16)
        dx_rows = lax.all_to_all(dx_cols, 'dp', 0, 1, tiled=True)
        dw_gate = jnp.einsum('td,tf->df', x_cols, gate_all, preferred_element_type=jnp.float32)
        dw_up = jnp.einsum('td,tf->df', x_cols, up_all, preferred_element_type=jnp.float32)
        dw_down = jnp.einsum('tf,td->fd', hidden_all, dy_cols, preferred_element_type=jnp.float32)
        return y_rows, dx_rows, dw_gate, dw_up, dw_down

    row_spec = P('dp', None)
    weight_spec = P('dp', 'tp')
    down_spec = P('tp', 'dp')
    return jax.shard_map(device_pass, mesh=mesh,
                         in_specs=(row_spec, weight_spec, weight_spec, down_spec, row_spec),
                         out_specs=(row_spec, row_spec, weight_spec, weight_spec, down_spec),
                         check_vma=False)
```

profile of v0, /device:TPU:1, one launch (start us, length us, event | category | flops | bytes accessed | tf_op | source)
XLA Modules:
  0.0 219.4 jit_solution(17930176059319010197)
XLA Ops:
  7.2 1.2 copy.23
  8.4 5.0 %all_to_all.76 = bf16[64,2,1536]{2,0,1:T(8,128)(2,1)S(1)} all-to-all(bf16[64,2,1536]{2,0,1:T(8,128)(2,1)S(1)} %bitcast.54), channel_id=1, replica_groups=mesh['tp'=64,'dp'=2] {'dp'}, dimensions={1} | all-to-all | bytes 786432 | tf_op jit(solution)/shard_map/all_to_all | solution.py:9
  13.5 1.1 fusion.2
  14.7 1.1 fusion.1
  15.9 4.0 %all_to_all.77 = bf16[64,2,1536]{2,0,1:T(8,128)(2,1)S(1)} all-to-all(bf16[64,2,1536]{2,0,1:T(8,128)(2,1)S(1)} %bitcast.55), channel_id=1, replica_groups=mesh['tp'=64,'dp'=2] {'dp'}, dimensions={1} | all-to-all | bytes 786432 | tf_op jit(solution)/shard_map/all_to_all | solution.py:21
  19.9 1.2 fusion.4
  21.2 6.5 %reduce-scatter.6.cloned.1.call-done = f32[64,384]{1,0:T(8,128)} async-done(((f32[128,384]{1,0:T(8,128)}), f32[64,384]{1,0:T(8,128)}) %reduce-scatter.6.cloned.1.call-update) | async-done | bytes 98320 | tf_op jit(solution)/shard_map/reduce_scatter | solution.py:13
  27.7 14.6 %reduce-scatter.4.cloned.1.call-done = f32[64,384]{1,0:T(8,128)} async-done(((f32[128,384]{1,0:T(8,128)}), f32[64,384]{1,0:T(8,128)}) %reduce-scatter.4.cloned.1.call-update) | async-done | bytes 98320 | tf_op jit(solution)/shard_map/reduce_scatter | solution.py:12
  42.3 14.6 %reduce-scatter.8.cloned.1.call-done = f32[64,384]{1,0:T(8,128)} async-done(((f32[128,384]{1,0:T(8,128)}), f32[64,384]{1,0:T(8,128)}) %reduce-scatter.8.cloned.1.call-update) | async-done | bytes 98320 | tf_op jit(solution)/shard_map/reduce_scatter | solution.py:23
  56.9 1.0 multiply_convert_fusion
  57.9 1.9 all_gather.11
  59.8 1.9 all_gather.10
  61.7 1.9 all_gather.9
  63.5 1.3 fusion.3
  66.1 1.4 convolution_add_fusion
  67.5 1.9 convolution_bitcast_fusion
  69.4 3.0 %copy.15 = f32[1536,384]{1,0:T(8,128)} copy(f32[1536,384]{0,1:T(8,128)} %convolution_bitcast_fusion) | data formatting | bytes 4718592
  72.4 1.9 convolution_bitcast_fusion.1
  74.3 3.0 %copy.14 = f32[1536,384]{1,0:T(8,128)} copy(f32[1536,384]{0,1:T(8,128)} %convolution_bitcast_fusion.1) | data formatting | bytes 4718592
  77.3 1.9 fusion.6
  79.2 120.0 %all-reduce.3.cloned.1.call-done = (f32[128,1536]{1,0:T(8,128)}, f32[128,1536]{1,0:T(8,128)}) async-done(((f32[128,1536]{1,0:T(8,128)}, f32[128,1536]{1,0:T(8,128)}), (f32[128,1536]{1,0:T(8,128)}, f32[128,1536]{1,0:T(8,128)})) %all-reduce.3.cloned.1.call-update) | async-done | bytes 1572880 | tf_op jit(solution)/shard_map/psum | solution.py:19
  199.2 1.2 add_convert_fusion.1
  200.4 6.7 %all_to_all.78 = bf16[2,64,1536]{2,1,0:T(8,128)(2,1)S(1)} all-to-all(bf16[2,64,1536]{2,1,0:T(8,128)(2,1)S(1)} %bitcast.56), channel_id=1, replica_groups=mesh['tp'=64,'dp'=2] {'dp'}, dimensions={0} | all-to-all | bytes 786432 | tf_op jit(solution)/shard_map/all_to_all | solution.py:20
  208.0 4.1 %all_to_all.79 = bf16[2,64,1536]{2,1,0:T(8,128)(2,1)S(1)} all-to-all(bf16[2,64,1536]{2,1,0:T(8,128)(2,1)S(1)} %bitcast.57), channel_id=1, replica_groups=mesh['tp'=64,'dp'=2] {'dp'}, dimensions={0} | all-to-all | bytes 786432 | tf_op jit(solution)/shard_map/all_to_all | solution.py:31
  (25 shorter events, 3.3 us)
Async XLA Ops:
  7.2 12.8 %copy-start = (bf16[384,1536]{1,0:T(8,128)(2,1)S(1)}, bf16[384,1536]{1,0:T(8,128)(2,1)}, u32[]{:S(2)}) copy-start(bf16[384,1536]{1,0:T(8,128)(2,1)} %param.8) | copy-start | bytes 3538948
  7.2 20.5 %reduce-scatter.6.cloned.1.call-start = ((), (), s32[]{:S(2)}) async-start(), calls=%async_computation.8 | async-start | bytes 294912 | tf_op jit(solution)/shard_map/reduce_scatter | solution.py:13
  7.2 6.2 %copy-start.2 = (bf16[1536,384]{1,0:T(8,128)(2,1)S(1)}, bf16[1536,384]{1,0:T(8,128)(2,1)}, u32[]{:S(2)}) copy-start(bf16[1536,384]{1,0:T(8,128)(2,1)} %param.7) | copy-start | bytes 3538948
  13.5 1.3 copy-start.1
  14.5 1.3 copy-start.5
  14.5 27.7 %reduce-scatter.4.cloned.1.call-start = ((), (), s32[]{:S(2)}) async-start(), calls=%async_computation.7 | async-start | bytes 294912 | tf_op jit(solution)/shard_map/reduce_scatter | solution.py:12
  15.8 41.1 %reduce-scatter.8.cloned.1.call-start = ((), (), s32[]{:S(2)}) async-start(), calls=%async_computation.9 | async-start | bytes 294912 | tf_op jit(solution)/shard_map/reduce_scatter | solution.py:23
  21.2 178.0 %all-reduce.3.cloned.1.call-start = ((), (), s32[]{:S(2)}) async-start(), calls=%async_computation.10 | async-start | bytes 3145728 | tf_op jit(solution)/shard_map/psum | solution.py:19
  64.8 1.3 copy-start.3
  200.4 7.5 %copy-start.4 = (f32[128,1536]{1,0:T(8,128)S(1)}, f32[128,1536]{1,0:T(8,128)}, u32[]{:S(2)}) copy-start(f32[128,1536]{1,0:T(8,128)} %get-tuple-element.11) | copy-start | bytes 2359300
Sparse Core Ops, SparseCore 0:
  14.7 12.9 reduce-scatter.5
  30.6 11.6 reduce-scatter.3
  45.2 11.6 reduce-scatter.7
  67.6 131.5 all-reduce.2
where the time goes:
time: 220 us; the launch traced here: 219 us
  waiting for transfers between devices  156 us (71%)
  blocking collectives  25.5 us (12%)
  between operations  13.8 us (6%)
  matrix products  12.1 us (6%)
  local copies, waits for them, and re-layouts  9.75 us (4%)
  other arithmetic  2.34 us (1%)
    psum x1, waiting for transfers between devices, device_pass(): lax.psum(out_part, 'tp')  120 us
    reduce_scatter x1, waiting for transfers between devices, device_pass(): lax.psum_scatter(gate_part, 'dp', scatter_dimension=0, tiled=True)  14.6 us
    reduce_scatter x1, waiting for transfers between devices, device_pass(): grad_h = lax.psum_scatter(grad_part, 'dp', scatter_dimension=0, tiled=True)  14.6 us
    unnamed x14, local copies, waits for them, and re-layouts  7.01 us
    all_to_all x1, blocking collectives, device_pass(): y_rows = lax.all_to_all(y_cols, 'dp', 0, 1, tiled=True)  6.73 us
    reduce_scatter x1, waiting for transfers between devices, device_pass(): up_pre = lax.psum_scatter(up_part, 'dp', scatter_dimension=0, tiled=True)  6.48 us
    all_to_all x1, blocking collectives, device_pass(): x_cols = lax.all_to_all(x_rows, 'dp', 1, 0, tiled=True)  5.04 us
  transfers between devices with their start and end apart: 4, of which 4 were waited for; matrix products, arithmetic and copies ran while one was open for 6% of the time, Pallas kernels for 0%

commit v1 on v0

v1 whole, which is shorter than its diff:
```python
import functools

import jax
import jax.numpy as jnp
from jax import lax
from jax.experimental import pallas as pl
from jax.experimental.pallas import tpu as pltpu
from jax.sharding import PartitionSpec as P

F32, BF16 = jnp.float32, jnp.bfloat16
ROWS, WIDTH, HALF, HID = 64, 3072, 1536, 384
PLANE = [(o2, o3) for o3 in range(4) for o2 in range(4) if o2 or o3]


def nt_dot(lhs, rhs):
    return lax.dot_general(lhs, rhs, (((1,), (1,)), ((), ())), preferred_element_type=F32)


def tn_dot(lhs, rhs):
    return lax.dot_general(lhs, rhs, (((0,), (0,)), ((), ())), preferred_element_type=F32)


def layer_kernel(x_hbm, wg_hbm, wu_hbm, wd_hbm, dy_hbm,
                 xc, dyc, hid, dga, dup, gath,
                 xv, dyv, wg, wu, wd, part, rpart, psum, recv1, mid, recv2, tiles15,
                 ld, xs, xr, ps, pr, s1s, s1r, s2s, s2r, s3s, s3r, s4s, s4r):
    t, c = lax.axis_index("tp"), lax.axis_index("dp")
    pos = [lax.rem(t, 4), lax.rem(t // 4, 4), t // 16]
    step = [1, 4, 16]
    delta = [[0 if o == 0 else (lax.rem(pos[d] + o, 4) - pos[d]) * step[d] for o in range(4)] for d in range(3)]

    def remote(src, dst, send, recv, tp, core):
        pltpu.make_async_remote_copy(src_ref=src, dst_ref=dst, send_sem=send, recv_sem=recv,
                                     device_id=(tp, core), device_id_type=pl.DeviceIdType.MESH).start()

    def wait_bytes(ref, sem):
        pltpu.make_async_copy(ref, ref, sem).wait()

    mine = pl.ds(pl.multiple_of(c * HALF, HALF), HALF)
    other = pl.ds(pl.multiple_of((1 - c) * HALF, HALF), HALF)
    own_rows, peer_rows = pl.ds(0, ROWS), pl.ds(ROWS, ROWS)
    loads = [pltpu.make_async_copy(x_hbm, xv, ld.at[0]),
             pltpu.make_async_copy(dy_hbm, dyv, ld.at[1]),
             pltpu.make_async_copy(x_hbm.at[:, mine], xc.at[own_rows], ld.at[2]),
             pltpu.make_async_copy(wg_hbm, wg, ld.at[3]),
             pltpu.make_async_copy(wu_hbm, wu, ld.at[4]),
             pltpu.make_async_copy(dy_hbm.at[:, mine], dyc.at[own_rows], ld.at[5]),
             pltpu.make_async_copy(wd_hbm, wd, ld.at[6])]
    barrier = pltpu.get_barrier_semaphore()
    pl.semaphore_signal(barrier, 1, device_id=(t, 1 - c), device_id_type=pl.DeviceIdType.MESH)
    for d in range(3):
        for o in range(1, 4):
            pl.semaphore_signal(barrier, 1, device_id=(t + delta[d][o], c), device_id_type=pl.DeviceIdType.MESH)
    for cp in loads:
        cp.start()
    loads[0].wait()
    loads[1].wait()
    pl.semaphore_wait(barrier, 10)

    remote(xv.at[:, other], xc.at[peer_rows], xs.at[0], xr.at[0], t, 1 - c)
    remote(dyv.at[:, other], dyc.at[peer_rows], xs.at[1], xr.at[1], t, 1 - c)

    def send_part(m, val):
        part[m, 1] = val[:ROWS]
        part[m, 0] = val[ROWS:]
        remote(part.at[m], rpart.at[m], ps.at[m], pr.at[m], t, 1 - c)

    loads[2].wait()
    loads[3].wait()
    wait_bytes(xc.at[peer_rows], xr.at[0])
    send_part(0, jnp.dot(xc[...], wg[...], preferred_element_type=F32))
    loads[4].wait()
    send_part(1, jnp.dot(xc[...], wu[...], preferred_element_type=F32))
    loads[5].wait()
    loads[6].wait()
    wait_bytes(dyc.at[peer_rows], xr.at[1])
    send_part(2, nt_dot(dyc[...], wd[...]))

    def full(m, e):
        return part[m, 1 - e] + rpart[m, e]

    def send1(j, a):
        for o in range(4):
            for e in range(2):
                if o or e:
                    slot = (o - 1) * 2 + e if o else 6
                    k = lax.rem(pos[j] + o, 4)
                    remote(psum.at[j, k, e, a], recv1.at[j, slot, a], s1s, s1r.at[j], t + delta[j][o],
                           1 - c if e else c)

    def put(j, a, val):
        for e in range(2):
            for r in range(4):
                for q in range(4):
                    psum[j, r, e, a, q] = val[e * 64 + r * 16:e * 64 + r * 16 + 16, q * 128:q * 128 + 128]

    wait_bytes(rpart.at[0], pr.at[0])
    wait_bytes(rpart.at[1], pr.at[1])
    for e in range(2):
        gate = full(0, e)
        hid[e * ROWS:(e + 1) * ROWS, :] = (gate * jax.nn.sigmoid(gate) * full(1, e)).astype(BF16)
    for j in range(3):
        put(j, 0, jnp.dot(hid[...], wd[:, j * 512:(j + 1) * 512], preferred_element_type=F32))
        send1(j, 0)
    wait_bytes(rpart.at[2], pr.at[2])
    for e in range(2):
        gate, up, grad = full(0, e), full(1, e), full(2, e)
        sig = jax.nn.sigmoid(gate)
        rows = slice(e * ROWS, (e + 1) * ROWS)
        dga[rows, :] = (grad * up * sig * (1.0 + gate * (1.0 - sig))).astype(BF16)
        dup[rows, :] = (grad * (gate * sig)).astype(BF16)
    for j in range(3):
        cols = slice(j * 512, (j + 1) * 512)
        put(j, 1, nt_dot(dga[...], wg[cols, :]) + nt_dot(dup[...], wu[cols, :]))
        send1(j, 1)

    def sum1_send2(j):
        d2, d3 = (j + 1) % 3, (j + 2) % 3
        mid[j, 0] = psum[j, pos[j], 0] + recv1[j, 0] + recv1[j, 2] + recv1[j, 4]
        mid[j, 1] = recv1[j, 6] + recv1[j, 1] + recv1[j, 3] + recv1[j, 5]
        for n, (o2, o3) in enumerate(PLANE):
            i2, i3 = lax.rem(pos[d2] + o2, 4), lax.rem(pos[d3] + o3, 4)
            remote(mid.at[j, lax.rem(i3 // 2 + c, 2), lax.rem(i3, 2), i2], recv2.at[j, n], s2s, s2r.at[j],
                   t + delta[d2][o2] + delta[d3][o3], c)

    wait_bytes(recv1.at[0], s1r.at[0])
    wait_bytes(recv1.at[1], s1r.at[1])
    sum1_send2(0)
    sum1_send2(1)
    wait_bytes(recv1.at[2], s1r.at[2])
    sum1_send2(2)

    for j in range(3):
        d2, d3 = (j + 1) % 3, (j + 2) % 3
        i1, i2, i3 = pos[j], pos[d2], pos[d3]
        half, which = i3 // 2, lax.rem(i3, 2)
        rows = pl.ds(pl.multiple_of(i1 * 16, 16), 16)
        cols = pl.ds(pl.multiple_of(half * HALF + j * 512 + i2 * 128, 128), 128)
        base = jnp.where(which == 0, xv[rows, cols].astype(F32), dyv[rows, cols].astype(F32))
        wait_bytes(recv2.at[j], s2r.at[j])
        total = mid[j, lax.rem(half + c, 2), which, i2]
        for n in range(15):
            total += recv2[j, n]
        gath[j, i1, i3, i2] = (base + total).astype(BF16)
        for o2, o3 in PLANE:
            remote(gath.at[j, i1, i3, i2], gath.at[j, i1, i3, i2], s3s.at[j], s3r.at[j],
                   t + delta[d2][o2] + delta[d3][o3], c)
    for j in range(3):
        wait_bytes(tiles15, s3r.at[j])
        for o in range(1, 4):
            remote(gath.at[j, pos[j]], gath.at[j, pos[j]], s4s, s4r.at[j], t + delta[j][o], c)
    wait_bytes(xv.at[:, other], xs.at[0])
    wait_bytes(dyv.at[:, other], xs.at[1])
    for m in range(3):
        wait_bytes(part.at[m], ps.at[m])
        wait_bytes(tiles15, s3s.at[m])
    wait_bytes(recv1, s1s)
    wait_bytes(recv2, s2s)
    for j in range(3):
        wait_bytes(gath.at[j, 0:3], s4r.at[j])
    wait_bytes(gath.at[:, 0:3], s4s)


def grad_kernel(xc, dyc, hid, dga, dup, gath, y_out, dx_out, dwg, dwu, dwd):
    i = pl.program_id(0)
    half, j = i // 3, lax.rem(i, 3)
    for a, out in enumerate((y_out, dx_out)):
        for r in range(4):
            for q in range(4):
                out[r * 16:(r + 1) * 16, q * 128:(q + 1) * 128] = gath[j, r, half * 2 + a, q]
    cols = pl.ds(pl.multiple_of(i * 256, 256), 256)
    xt = xc[:, cols]
    dwg[...] = tn_dot(xt, dga[...])
    dwu[...] = tn_dot(xt, dup[...])
    dwd[...] = tn_dot(hid[...], dyc[:, cols])


def solution(mesh):
    vmem = pl.BlockSpec(memory_space=pltpu.VMEM)
    hbm = pl.BlockSpec(memory_space=pl.ANY)
    sds = jax.ShapeDtypeStruct

    def device_pass(x_rows, gate_blk, up_blk, down_blk, dy_rows):
        mids = pl.pallas_call(
            layer_kernel,
            name="layer",
            out_shape=[sds((128, HALF), BF16), sds((128, HALF), BF16), sds((128, HID), BF16), sds((128, HID), BF16),
                       sds((128, HID), BF16), sds((3, 4, 4, 4, 16, 128), BF16)],
            in_specs=[hbm] * 5,
            out_specs=[vmem] * 6,
            scratch_shapes=[
                pltpu.VMEM((ROWS, WIDTH), BF16), pltpu.VMEM((ROWS, WIDTH), BF16),
                pltpu.VMEM((HALF, HID), BF16), pltpu.VMEM((HALF, HID), BF16), pltpu.VMEM((HID, HALF), BF16),
                pltpu.VMEM((3, 2, ROWS, HID), F32), pltpu.VMEM((3, 2, ROWS, HID), F32),
                pltpu.VMEM((3, 4, 2, 2, 4, 16, 128), F32), pltpu.VMEM((3, 7, 2, 4, 16, 128), F32),
                pltpu.VMEM((3, 2, 2, 4, 16, 128), F32), pltpu.VMEM((3, 15, 16, 128), F32),
                pltpu.VMEM((15, 16, 128), BF16),
                pltpu.SemaphoreType.DMA((7,)), pltpu.SemaphoreType.DMA((2,)), pltpu.SemaphoreType.DMA((2,)),
                pltpu.SemaphoreType.DMA((3,)), pltpu.SemaphoreType.DMA((3,)),
                pltpu.SemaphoreType.DMA, pltpu.SemaphoreType.DMA((3,)),
                pltpu.SemaphoreType.DMA, pltpu.SemaphoreType.DMA((3,)),
                pltpu.SemaphoreType.DMA((3,)), pltpu.SemaphoreType.DMA((3,)),
                pltpu.SemaphoreType.DMA, pltpu.SemaphoreType.DMA((3,)),
            ],
            compiler_params=pltpu.CompilerParams(collective_id=0, has_side_effects=True),
        )(x_rows, gate_blk, up_blk, down_blk, dy_rows)
        return tuple(pl.pallas_call(
            grad_kernel,
            name="grads",
            grid=(6,),
            out_shape=[sds((ROWS, WIDTH), BF16), sds((ROWS, WIDTH), BF16), sds((HALF, HID), F32), sds((HALF, HID), F32),
                       sds((HID, HALF), F32)],
            in_specs=[vmem] * 6,
            out_specs=[pl.BlockSpec((ROWS, 512), lambda i: (0, i)), pl.BlockSpec((ROWS, 512), lambda i: (0, i)),
                       pl.BlockSpec((256, HID), lambda i: (i, 0)), pl.BlockSpec((256, HID), lambda i: (i, 0)),
                       pl.BlockSpec((HID, 256), lambda i: (0, i))],
        )(*mids))

    row_spec = P('dp', None)
    weight_spec = P('dp', 'tp')
    down_spec = P('tp', 'dp')
    return jax.shard_map(device_pass, mesh=mesh,
                         in_specs=(row_spec, weight_spec, weight_spec, down_spec, row_spec),
                         out_specs=(row_spec, row_spec, weight_spec, weight_spec, down_spec),
                         check_vma=False)
```

time: 220 us -> 42.6 us (0.19)
  the two profiles are of different devices: /device:TPU:1 before, /device:TPU:0 now
where the time goes in v1:
time: 42.6 us; the launch traced here: 42.4 us
  Pallas kernels  41.8 us (98%)
  between operations  0.64 us (2%)
    pallas_call x1, Pallas kernels, device_pass(): pl.pallas_call(layer_kernel, name='layer', out_shape=[sds((128, HALF), BF...  35.9 us
    pallas_call x1, Pallas kernels, device_pass(): pl.pallas_call(grad_kernel, name='grads', grid=(6,), out_shape=[sds((ROWS...  5.85 us

profile of v1, /device:TPU:0, one launch (start us, length us, event | category | flops | bytes accessed | tf_op | source)
XLA Modules:
  0.0 42.4 jit_solution(7347273730708776173)
XLA Ops:
  0.6 35.9 %layer.1 = (bf16[128,1536]{1,0:T(8,128)(2,1)}, bf16[128,1536]{1,0:T(8,128)(2,1)}, bf16[128,384]{1,0:T(8,128)(2,1)}, bf16[128,384]{1,0:T(8,128)(2,1)}, bf16[128,3...) custom-call(bf16[64,3072]{1,0:T(8,128)(2,1)} %x_hbm.1, bf16[1536,384]{1,0:T(8,128)(2,1)} %wg_hbm.1, ...), custom_call_target="tpu_custom_call" | custom-call | tf_op jit(solution)/shard_map/layer/pallas_call | solution.py:184
  36.6 5.9 %grads.1 = (bf16[64,3072]{1,0:T(8,128)(2,1)}, bf16[64,3072]{1,0:T(8,128)(2,1)}, f32[1536,384]{1,0:T(8,128)}, f32[1536,384]{1,0:T(8,128)}, f32[384,1536]{1,0:T(8,128)}) custom-call(bf16[128,1536]{1,0:T(8,128)(2,1)} %get-tuple-element.11.xc, bf16[128,1536]{1,0:T(8,128)(2,1)} %get-tuple-element.12.dyc, bf16[128,384]{1,0:T(8,128)(2,1)} %get-tuple-element.13.hid, ...), custom_call_target="tpu_custom_call" | custom-call | tf_op jit(solution)/shard_map/grads/pallas_call | solution.py:207

commit v2 on v1

--- a/solution.py
+++ b/solution.py
@@ -1,5 +1,3 @@
-import functools
-
 import jax
 import jax.numpy as jnp
 from jax import lax
@@ -21,8 +19,8 @@
 
 
 def layer_kernel(x_hbm, wg_hbm, wu_hbm, wd_hbm, dy_hbm,
-                 xc, dyc, hid, dga, dup, gath,
-                 xv, dyv, wg, wu, wd, part, rpart, psum, recv1, mid, recv2, tiles15,
+                 dwg, dwu, dwd, gath,
+                 xc, dyc, hid, dga, dup, xv, dyv, wg, wu, wd, part, rpart, psum, recv1, mid, recv2, tiles,
                  ld, xs, xr, ps, pr, s1s, s1r, s2s, s2r, s3s, s3r, s4s, s4r):
     t, c = lax.axis_index("tp"), lax.axis_index("dp")
     pos = [lax.rem(t, 4), lax.rem(t // 4, 4), t // 16]
@@ -85,7 +83,7 @@
                 if o or e:
                     slot = (o - 1) * 2 + e if o else 6
                     k = lax.rem(pos[j] + o, 4)
-                    remote(psum.at[j, k, e, a], recv1.at[j, slot, a], s1s, s1r.at[j], t + delta[j][o],
+                    remote(psum.at[j, k, e, a], recv1.at[j, a, slot], s1s, s1r.at[j, a], t + delta[j][o],
                            1 - c if e else c)
 
     def put(j, a, val):
@@ -113,108 +111,141 @@
         cols = slice(j * 512, (j + 1) * 512)
         put(j, 1, nt_dot(dga[...], wg[cols, :]) + nt_dot(dup[...], wu[cols, :]))
         send1(j, 1)
-
-    def sum1_send2(j):
+    for i in range(6):
+        cols = slice(i * 256, (i + 1) * 256)
+        dwd[:, cols] = tn_dot(hid[...], dyc[:, cols])
+    for i in range(6):
+        cols = slice(i * 256, (i + 1) * 256)
+        dwg[cols, :] = tn_dot(xc[:, cols], dga[...])
+        dwu[cols, :] = tn_dot(xc[:, cols], dup[...])
+
+    def stage2(j, a):
         d2, d3 = (j + 1) % 3, (j + 2) % 3
-        mid[j, 0] = psum[j, pos[j], 0] + recv1[j, 0] + recv1[j, 2] + recv1[j, 4]
-        mid[j, 1] = recv1[j, 6] + recv1[j, 1] + recv1[j, 3] + recv1[j, 5]
-        for n, (o2, o3) in enumerate(PLANE):
-            i2, i3 = lax.rem(pos[d2] + o2, 4), lax.rem(pos[d3] + o3, 4)
-            remote(mid.at[j, lax.rem(i3 // 2 + c, 2), lax.rem(i3, 2), i2], recv2.at[j, n], s2s, s2r.at[j],
-                   t + delta[d2][o2] + delta[d3][o3], c)
-
-    wait_bytes(recv1.at[0], s1r.at[0])
-    wait_bytes(recv1.at[1], s1r.at[1])
-    sum1_send2(0)
-    sum1_send2(1)
-    wait_bytes(recv1.at[2], s1r.at[2])
-    sum1_send2(2)
-
-    for j in range(3):
+        for e in range(2):
+            own = recv1[j, a, 6] if e else psum[j, pos[j], 0, a]
+            mid[j, a, e] = own + recv1[j, a, e] + recv1[j, a, 2 + e] + recv1[j, a, 4 + e]
+        odd = lax.rem(pos[d3] + a, 2)
+        for h in range(2):
+            o3 = odd + 2 * h
+            i3 = lax.rem(pos[d3] + o3, 4)
+            for o2 in range(4):
+                def send():
+                    remote(mid.at[j, a, lax.rem(i3 // 2 + c, 2), lax.rem(pos[d2] + o2, 4)],
+                           recv2.at[j, o3 * 4 + o2 - 1], s2s, s2r.at[j],
+                           t + delta[d2][o2] + (i3 - pos[d3]) * step[d3], c)
+                if h or o2:
+                    send()
+                else:
+                    pl.when(odd == 1)(send)
+
+    for a in range(2):
+        wait_bytes(recv1.at[0, a], s1r.at[0, a])
+        wait_bytes(recv1.at[1, a], s1r.at[1, a])
+        stage2(0, a)
+        stage2(1, a)
+        wait_bytes(recv1.at[2, a], s1r.at[2, a])
+        stage2(2, a)
+
+    def stage3(j, a):
         d2, d3 = (j + 1) % 3, (j + 2) % 3
-        i1, i2, i3 = pos[j], pos[d2], pos[d3]
-        half, which = i3 // 2, lax.rem(i3, 2)
+        i1, i2, half = pos[j], pos[d2], pos[d3] // 2
         rows = pl.ds(pl.multiple_of(i1 * 16, 16), 16)
         cols = pl.ds(pl.multiple_of(half * HALF + j * 512 + i2 * 128, 128), 128)
-        base = jnp.where(which == 0, xv[rows, cols].astype(F32), dyv[rows, cols].astype(F32))
+        base = (dyv if a else xv)[rows, cols].astype(F32)
         wait_bytes(recv2.at[j], s2r.at[j])
-        total = mid[j, lax.rem(half + c, 2), which, i2]
+        total = mid[j, a, lax.rem(half + c, 2), i2]
         for n in range(15):
             total += recv2[j, n]
-        gath[j, i1, i3, i2] = (base + total).astype(BF16)
+        gath[j, i1, a, half, i2] = (base + total).astype(BF16)
         for o2, o3 in PLANE:
-            remote(gath.at[j, i1, i3, i2], gath.at[j, i1, i3, i2], s3s.at[j], s3r.at[j],
+            remote(gath.at[j, i1, a, half, i2], gath.at[j, i1, a, half, i2], s3s.at[j], s3r.at[j, a],
                    t + delta[d2][o2] + delta[d3][o3], c)
-    for j in range(3):
-        wait_bytes(tiles15, s3r.at[j])
-        for o in range(1, 4):
-            remote(gath.at[j, pos[j]], gath.at[j, pos[j]], s4s, s4r.at[j], t + delta[j][o], c)
+
+    for a in range(2):
+        for j in range(3):
+            pl.when(lax.rem(pos[(j + 2) % 3], 2) == a)(lambda: stage3(j, a))
+    for a in range(2):
+        for j in range(3):
+            owner = lax.rem(pos[(j + 2) % 3], 2) == a
+            pl.when(owner)(lambda: wait_bytes(tiles.at[0:7], s3r.at[j, a]))
+            pl.when(jnp.logical_not(owner))(lambda: wait_bytes(tiles.at[0:8], s3r.at[j, a]))
+            for o in range(1, 4):
+                remote(gath.at[j, pos[j], a], gath.at[j, pos[j], a], s4s, s4r.at[j, a], t + delta[j][o], c)
     wait_bytes(xv.at[:, other], xs.at[0])
     wait_bytes(dyv.at[:, other], xs.at[1])
     for m in range(3):
         wait_bytes(part.at[m], ps.at[m])
-        wait_bytes(tiles15, s3s.at[m])
+        wait_bytes(tiles, s3s.at[m])
     wait_bytes(recv1, s1s)
     wait_bytes(recv2, s2s)
-    for j in range(3):
-        wait_bytes(gath.at[j, 0:3], s4r.at[j])
+    for a in range(2):
+        for j in range(3):
+            wait_bytes(gath.at[j, 0:3, a], s4r.at[j, a])
     wait_bytes(gath.at[:, 0:3], s4s)
 
 
-def grad_kernel(xc, dyc, hid, dga, dup, gath, y_out, dx_out, dwg, dwu, dwd):
-    i = pl.program_id(0)
-    half, j = i // 3, lax.rem(i, 3)
+def flush_kernel(dwg, dwu, dwd, gath, y_out, dx_out, dwg_out, dwu_out, dwd_out, rows, sem):
+    copies = []
+    for n, (src, dst) in enumerate(((dwg, dwg_out), (dwu, dwu_out), (dwd, dwd_out))):
+        size = src.shape[0] // 4
+        for k in range(4):
+            part = pl.ds(k * size, size)
+            copies.append(pltpu.make_async_copy(src.at[part], dst.at[part], sem.at[4 * n + k]))
+            copies[-1].start()
     for a, out in enumerate((y_out, dx_out)):
-        for r in range(4):
-            for q in range(4):
-                out[r * 16:(r + 1) * 16, q * 128:(q + 1) * 128] = gath[j, r, half * 2 + a, q]
-    cols = pl.ds(pl.multiple_of(i * 256, 256), 256)
-    xt = xc[:, cols]
-    dwg[...] = tn_dot(xt, dga[...])
-    dwu[...] = tn_dot(xt, dup[...])
-    dwd[...] = tn_dot(hid[...], dyc[:, cols])
+        for j in range(3):
+            for half in range(2):
+                for r in range(4):
+                    for q in range(4):
+                        col = half * HALF + j * 512 + q * 128
+                        rows[a, r * 16:(r + 1) * 16, col:col + 128] = gath[j, r, a, half, q]
+        copies.append(pltpu.make_async_copy(rows.at[a], out, sem.at[12 + a]))
+        copies[-1].start()
+    for cp in copies:
+        cp.wait()
 
 
 def solution(mesh):
     vmem = pl.BlockSpec(memory_space=pltpu.VMEM)
-    hbm = pl.BlockSpec(memory_space=pl.ANY)
+    hbm = pl.BlockSpec(memory_space=pltpu.HBM)
     sds = jax.ShapeDtypeStruct
 
     def device_pass(x_rows, gate_blk, up_blk, down_blk, dy_rows):
-        mids = pl.pallas_call(
+        results = pl.pallas_call(
             layer_kernel,
             name="layer",
-            out_shape=[sds((128, HALF), BF16), sds((128, HALF), BF16), sds((128, HID), BF16), sds((128, HID), BF16),
-                       sds((128, HID), BF16), sds((3, 4, 4, 4, 16, 128), BF16)],
+            out_shape=[pltpu.VMEM((HALF, HID), F32), pltpu.VMEM((HALF, HID), F32), pltpu.VMEM((HID, HALF), F32),
+                       pltpu.VMEM((3, 4, 2, 2, 4, 16, 128), BF16)],
             in_specs=[hbm] * 5,
-            out_specs=[vmem] * 6,
+            out_specs=[vmem] * 4,
             scratch_shapes=[
+                pltpu.VMEM((128, HALF), BF16), pltpu.VMEM((128, HALF), BF16),
+                pltpu.VMEM((128, HID), BF16), pltpu.VMEM((128, HID), BF16), pltpu.VMEM((128, HID), BF16),
                 pltpu.VMEM((ROWS, WIDTH), BF16), pltpu.VMEM((ROWS, WIDTH), BF16),
                 pltpu.VMEM((HALF, HID), BF16), pltpu.VMEM((HALF, HID), BF16), pltpu.VMEM((HID, HALF), BF16),
                 pltpu.VMEM((3, 2, ROWS, HID), F32), pltpu.VMEM((3, 2, ROWS, HID), F32),
-                pltpu.VMEM((3, 4, 2, 2, 4, 16, 128), F32), pltpu.VMEM((3, 7, 2, 4, 16, 128), F32),
+                pltpu.VMEM((3, 4, 2, 2, 4, 16, 128), F32), pltpu.VMEM((3, 2, 7, 4, 16, 128), F32),
                 pltpu.VMEM((3, 2, 2, 4, 16, 128), F32), pltpu.VMEM((3, 15, 16, 128), F32),
                 pltpu.VMEM((15, 16, 128), BF16),
                 pltpu.SemaphoreType.DMA((7,)), pltpu.SemaphoreType.DMA((2,)), pltpu.SemaphoreType.DMA((2,)),
                 pltpu.SemaphoreType.DMA((3,)), pltpu.SemaphoreType.DMA((3,)),
+                pltpu.SemaphoreType.DMA, pltpu.SemaphoreType.DMA((3, 2)),
                 pltpu.SemaphoreType.DMA, pltpu.SemaphoreType.DMA((3,)),
-                pltpu.SemaphoreType.DMA, pltpu.SemaphoreType.DMA((3,)),
-                pltpu.SemaphoreType.DMA((3,)), pltpu.SemaphoreType.DMA((3,)),
-                pltpu.SemaphoreType.DMA, pltpu.SemaphoreType.DMA((3,)),
+                pltpu.SemaphoreType.DMA((3,)), pltpu.SemaphoreType.DMA((3, 2)),
+                pltpu.SemaphoreType.DMA, pltpu.SemaphoreType.DMA((3, 2)),
             ],
-            compiler_params=pltpu.CompilerParams(collective_id=0, has_side_effects=True),
+            compiler_params=pltpu.CompilerParams(collective_id=0, has_side_effects=True, vmem_limit_bytes=59000000),
         )(x_rows, gate_blk, up_blk, down_blk, dy_rows)
         return tuple(pl.pallas_call(
-            grad_kernel,
-            name="grads",
-            grid=(6,),
+            flush_kernel,
+            name="flush",
             out_shape=[sds((ROWS, WIDTH), BF16), sds((ROWS, WIDTH), BF16), sds((HALF, HID), F32), sds((HALF, HID), F32),
                        sds((HID, HALF), F32)],
-            in_specs=[vmem] * 6,
-            out_specs=[pl.BlockSpec((ROWS, 512), lambda i: (0, i)), pl.BlockSpec((ROWS, 512), lambda i: (0, i)),
-                       pl.BlockSpec((256, HID), lambda i: (i, 0)), pl.BlockSpec((256, HID), lambda i: (i, 0)),
-                       pl.BlockSpec((HID, 256), lambda i: (0, i))],
-        )(*mids))
+            in_specs=[vmem] * 4,
+            out_specs=[hbm] * 5,
+            scratch_shapes=[pltpu.VMEM((2, ROWS, WIDTH), BF16), pltpu.SemaphoreType.DMA((14,))],
+            compiler_params=pltpu.CompilerParams(vmem_limit_bytes=16 * 2**20),
+        )(*results))
 
     row_spec = P('dp', None)
     weight_spec = P('dp', 'tp')

time: 42.6 us -> 36.9 us (0.87)
  the two profiles are of different devices: /device:TPU:0 before, /device:TPU:1 now
where the time goes in v2:
time: 36.9 us; the launch traced here: 36.7 us
  Pallas kernels  36 us (98%)
  between operations  0.64 us (2%)
    pallas_call x1, Pallas kernels, device_pass(): pl.pallas_call(layer_kernel, name='layer', out_shape=[pltpu.VMEM((HALF, H...  32.8 us
    pallas_call x1, Pallas kernels, device_pass(): pl.pallas_call(flush_kernel, name='flush', out_shape=[sds((ROWS, WIDTH),...  3.25 us

profile of v2, /device:TPU:1, one launch (start us, length us, event | category | flops | bytes accessed | tf_op | source)
XLA Modules:
  0.0 36.7 jit_solution(17574749229818591002)
XLA Ops:
  0.6 32.8 %layer.1 = (f32[1536,384]{1,0:T(8,128)S(1)}, f32[1536,384]{1,0:T(8,128)S(1)}, f32[384,1536]{1,0:T(8,128)S(1)}, bf16[3,4,2,2,4,16,128]{6,5,4,3,2,1,0:T(8,128)(2,1)S(1)}) custom-call(bf16[64,3072]{1,0:T(8,128)(2,1)} %x_hbm.1, bf16[1536,384]{1,0:T(8,128)(2,1)} %wg_hbm.1, bf16[1536,384]{1,0:T(8,128)(2,1)} %wu_hbm.1, bf16[384,1536]{1,0:T(8,128)(2,1)} %wd_hbm.1, ...), custom_call_target="tpu_custom_call" | custom-call | tf_op jit(solution)/shard_map/layer/pallas_call | solution.py:214
  33.4 3.3 %flush.1 = (bf16[64,3072]{1,0:T(8,128)(2,1)}, bf16[64,3072]{1,0:T(8,128)(2,1)}, f32[1536,384]{1,0:T(8,128)}, f32[1536,384]{1,0:T(8,128)}, f32[384,1536]{1,0:T(8,128)}) custom-call(f32[1536,384]{1,0:T(8,128)S(1)} %get-tuple-element.9.dwg, f32[1536,384]{1,0:T(8,128)S(1)} %get-tuple-element.10.dwu, f32[384,1536]{1,0:T(8,128)S(1)} %get-tuple-element.11.dwd, ...), custom_call_target="tpu_custom_call" | custom-call | tf_op jit(solution)/shard_map/flush/pallas_call | solution.py:239
